TPU v7x, 32 devices: a whole 2x2x4 slice. The times are simulated.
32 devices in a mesh: ccd: 16 (over z, y, x), row: 2 (over core).
Axes of the slice: x: 2, y: 2, z: 4, core: 2. Of those that a mesh axis runs over, the one named last changes fastest.
Arguments:
- exposure: float32 [16, 48, 2048], P('ccd', 'row'), may hold values from -6 to 6
- row_shift: int32 [16], P('ccd'), may hold values from 0 to 7
- row_fraction: bfloat16 [16, 48], P('ccd', 'row'), may hold values from 0 to 1
- column_shift: int32 [16], P('ccd'), may hold values from 0 to 127
- column_fraction: bfloat16 [16, 2048], P('ccd'), may hold values from 0 to 1
- piece_width: int32 [16, 16], P('ccd'), may hold values from 1 to 128
- route_tile: int32 [16, 16], P('ccd'), may hold values from 0 to 15, as said below
- route_cell: int32 [16, 16], P('ccd'), may hold values from 0 to 31, as said below
- template: float32 [16, 48, 4096], P('ccd', 'row'), may hold values from -6 to 6
- match_kernel: bfloat16 [16, 41, 41], P('ccd'), may hold values from -0.15625 to 0.15625
- detection_kernel: bfloat16 [16, 15, 15], P('ccd'), may hold values from -0.375 to 0.375
Outputs:
- difference: float32 [16, 48, 4096], P('ccd', 'row')
- significance: float32 [16, 48, 4096], P('ccd', 'row')
- noise_level: float32 [], replicated
Inputs may be any that keep to these rules, and one draw needn't show every extreme that they name: Piece p of CCD c lands on tile route_tile[c, p]. Every tile receives at least one piece and at most 32 pieces in all; a quarter of the tiles receive exactly 32. No CCD puts more than 2 pieces on one tile, and some CCDs put exactly 2. `route_cell`: pieces that land on one tile fill different cells.
All inputs are finite; a program needn't handle non-finite values.
Results may differ from a plain program's by a relative error of at most 0.0044.
Values may be sent and summed in bfloat16 or wider, within the bound.
A program may use at most 128 MiB of HBM per device.

v0:
```python
import jax
import jax.numpy as jnp
from jax import lax
from jax.sharding import PartitionSpec as P

PW = 128
PAIR = 2
HALO = 8
KS = 41
DK = 15


stack_depth = 5


def extended_2(x, sides, width):
    for axis, dim in sides:
        size, length = (lax.axis_size(axis), x.shape[dim])
        up = [(i, (i + 1) % size) for i in range(size - 1)]
        down = [(j, i) for i, j in up]
        last = lax.slice_in_dim(x, length - width, length, axis=dim)
        first = lax.slice_in_dim(x, 0, width, axis=dim)
        before = lax.ppermute(last, axis, up)
        after = lax.ppermute(first, axis, down)
        x = jnp.concatenate([before, x, after], axis=dim)
    return x


def passed_along(block, axis, distance):
    devices = range(lax.axis_size(axis))
    route = [(i - distance, i) for i in devices if i - distance in devices]
    return lax.ppermute(block, axis, route)


def warp_columns(padded, column_offset, fraction):
    length = fraction.shape[-1]
    leftward = lax.dynamic_slice_in_dim(padded, column_offset, length, 1).astype(jnp.float32)
    rightward = lax.dynamic_slice_in_dim(padded, column_offset + 1, length, 1).astype(jnp.float32)
    weight = fraction.astype(jnp.float32)[None, :]
    return (1.0 - weight) * leftward + weight * rightward


def band_matrix(kernel):
    extent = kernel.shape[0]
    spread = jnp.arange(2 * PW, dtype=jnp.int32)[:, None] - jnp.arange(PW, dtype=jnp.int32)[None, :]
    picker = (spread[:, :, None] == jnp.arange(extent, dtype=jnp.int32)[None, None, :]).astype(
        jnp.bfloat16
    )
    return jnp.einsum("yd,kjd->ykj", kernel, picker, preferred_element_type=jnp.float32).astype(
        jnp.bfloat16
    )


def banded_filter(source, kernel, height):
    extent = kernel.shape[0]
    margin = extent // 2
    blocks_wide = source.shape[1] // PW
    widened = jnp.pad(source, ((0, 0), (margin, 2 * PW - margin)))
    blocked = widened.reshape(widened.shape[0], blocks_wide + 2, PW)
    windows = jnp.concatenate([blocked[:, :blocks_wide], blocked[:, 1 : blocks_wide + 1]], axis=2)
    banded = band_matrix(kernel)
    running = jnp.zeros((height, blocks_wide, PW), jnp.float32)
    for offset in range(0, extent, stack_depth):
        finish = min(offset + stack_depth, extent)
        stacked = jnp.stack(
            [windows[depth_row : depth_row + height] for depth_row in range(offset, finish)], axis=2
        )
        running = running + jnp.einsum(
            "rcgk,gkj->rcj", stacked, banded[offset:finish], preferred_element_type=jnp.float32
        )
    return running.reshape(height, blocks_wide * PW)


def match_template(template, match_kernel, height):
    rounded = template[0].astype(jnp.bfloat16)
    haloed = extended_2(rounded, (("row", 0),), KS // 2)
    return banded_filter(haloed, match_kernel[0], height)


def detection_pass(difference, detection_kernel, height):
    rounded = difference.astype(jnp.bfloat16)
    haloed = extended_2(rounded, (("row", 0),), DK // 2)
    return banded_filter(haloed, detection_kernel[0], height)


def noise_totals(square_sum, live_count):
    return lax.psum((square_sum, live_count), ("ccd", "row"))


def deliver_pieces(
    exposure,
    row_shift,
    row_fraction,
    column_shift,
    column_fraction,
    piece_width,
    route_tile,
    route_cell,
    cell_count,
):
    exposure_band = exposure[0]
    height = exposure_band.shape[0]
    columns = exposure_band.shape[1]
    pieces = columns // PW
    capacity = lax.axis_size("ccd") * PAIR
    below_rows = passed_along(exposure_band[:HALO], "row", -1)
    extended = jnp.concatenate([exposure_band, below_rows], axis=0)
    weight = row_fraction[0].astype(jnp.float32)[:, None]
    upper_rows = lax.dynamic_slice_in_dim(extended, row_shift[0], height, 0)
    lower_rows = lax.dynamic_slice_in_dim(extended, row_shift[0] + 1, height, 0)
    warped_rows = ((1.0 - weight) * upper_rows + weight * lower_rows).astype(jnp.bfloat16)
    padded = jnp.pad(warped_rows, ((0, 0), (0, PW)))
    piece_tile = route_tile[0]
    piece_cell = route_cell[0]
    widths = piece_width[0]
    order_index = jnp.arange(pieces, dtype=jnp.int32)
    earlier = (piece_tile[:, None] == piece_tile[None, :]) & (
        order_index[None, :] < order_index[:, None]
    )
    piece_rank = jnp.sum(earlier.astype(jnp.int32), axis=1)
    target = piece_tile * PAIR + piece_rank
    chooser = jnp.arange(capacity, dtype=jnp.int32)[:, None] == target[None, :]
    chooser_half = chooser.astype(jnp.bfloat16)
    sent_cell = jnp.sum(jnp.where(chooser, piece_cell[None, :] + 1, 0), axis=1) - 1
    sent_width = jnp.sum(jnp.where(chooser, widths[None, :], 0), axis=1)
    lane_index = jnp.arange(PW, dtype=jnp.int32)
    warped = warp_columns(padded, column_shift[0], column_fraction[0]).astype(jnp.bfloat16)
    keep_mask = (lane_index[None, :] < widths[:, None]).reshape(columns)
    warped = jnp.where(keep_mask[None, :], warped, jnp.zeros((), jnp.bfloat16))
    outgoing = jnp.einsum(
        "sp,rpj->srj",
        chooser_half,
        warped.reshape(height, pieces, PW),
        preferred_element_type=jnp.float32,
    ).astype(jnp.bfloat16)
    incoming, got_cell, got_width = (
        lax.all_to_all(outgoing, "ccd", split_axis=0, concat_axis=0, tiled=True),
        lax.all_to_all(sent_cell, "ccd", split_axis=0, concat_axis=0, tiled=True),
        lax.all_to_all(sent_width, "ccd", split_axis=0, concat_axis=0, tiled=True),
    )
    placer = jnp.arange(cell_count, dtype=jnp.int32)[:, None] == got_cell[None, :]
    science = jnp.einsum(
        "qs,srj->rqj", placer.astype(jnp.bfloat16), incoming, preferred_element_type=jnp.float32
    ).reshape(height, cell_count * PW)
    cell_width = jnp.sum(jnp.where(placer, got_width[None, :], 0), axis=1).astype(jnp.int32)
    live_mask = (lane_index[None, :] < cell_width[:, None]).reshape(cell_count * PW)
    return (science, live_mask, cell_width)


def on_device(
    exposure,
    row_shift,
    row_fraction,
    column_shift,
    column_fraction,
    piece_width,
    route_tile,
    route_cell,
    template,
    match_kernel,
    detection_kernel,
):
    height = exposure.shape[1]
    cell_count = template.shape[2] // PW
    science, live_mask, cell_width = deliver_pieces(
        exposure,
        row_shift,
        row_fraction,
        column_shift,
        column_fraction,
        piece_width,
        route_tile,
        route_cell,
        cell_count,
    )
    matched = match_template(template, match_kernel, height)
    difference = jnp.where(live_mask[None, :], science - matched, jnp.zeros((), jnp.float32))
    square_sum = jnp.sum(difference * difference)
    live_count = (height * jnp.sum(cell_width)).astype(jnp.float32)
    filtered = detection_pass(difference, detection_kernel, height)
    total_square, total_count = noise_totals(square_sum, live_count)
    noise_level = total_square / total_count
    detect_weights = detection_kernel[0].astype(jnp.float32)
    kernel_norm = jnp.sum(detect_weights * detect_weights)
    significance = filtered / jnp.sqrt(1.0 + noise_level * kernel_norm)
    return (difference[None], significance[None], noise_level)


def solution(mesh):
    return jax.shard_map(
        on_device,
        mesh=mesh,
        in_specs=(
            P("ccd", "row", None),
            P("ccd"),
            P("ccd", "row"),
            P("ccd"),
            P("ccd", None),
            P("ccd", None),
            P("ccd", None),
            P("ccd", None),
            P("ccd", "row", None),
            P("ccd", None, None),
            P("ccd", None, None),
        ),
        out_specs=(P("ccd", "row", None), P("ccd", "row", None), P()),
        check_vma=False,
    )
```

profile of v0, /device:TPU:0, one launch (start us, length us, event | category | flops | bytes accessed | tf_op | source)
XLA Modules:
  0.0 126.3 jit_solution(17106949905012191423)
XLA Ops:
  0.6 1.0 convert_element_type.82
  2.5 3.1 %collective-permute-start.1 = (bf16[20,4096]{1,0:T(8,128)(2,1)}, bf16[20,4096]{1,0:T(8,128)(2,1)}, u32[]{:S(2)}, u32[]{:S(2)}) collective-permute-start(bf16[20,4096]{1,0:T(8,128)(2,1)} %get-tuple-element.53), channel_id=1, source_target_pairs={{0,1},{2,3},{4,5},{6,7},{8,9},{10,11},{12,13},{14,15},{16,17},{18,... | collective-permute-start | bytes 491528 | tf_op jit(solution)/shard_map/ppermute | solution.py:23
  5.5 1.3 %collective-permute-start.2 = (bf16[20,4096]{1,0:T(8,128)(2,1)}, bf16[20,4096]{1,0:T(8,128)(2,1)}, u32[]{:S(2)}, u32[]{:S(2)}) collective-permute-start(bf16[20,4096]{1,0:T(8,128)(2,1)} %get-tuple-element.54), channel_id=1, source_target_pairs={{1,0},{3,2},{5,4},{7,6},{9,8},{11,10},{13,12},{15,14},{17,16},{19,... | collective-permute-start | bytes 491528 | tf_op jit(solution)/shard_map/ppermute | solution.py:24
  6.8 1.5 %slice_bitcast_fusion.11 = f32[8,2048]{1,0:T(8,128)} fusion(f32[1,24,2048]{2,1,0:T(8,128)} %param.11), kind=kLoop, calls=%fused_computation.369 | loop fusion | bytes 131072 | tf_op jit(solution)/shard_map/slice | solution.py:106
  8.3 1.3 %collective-permute-start = (f32[8,2048]{1,0:T(8,128)}, f32[8,2048]{1,0:T(8,128)}, u32[]{:S(2)}, u32[]{:S(2)}) collective-permute-start(f32[8,2048]{1,0:T(8,128)} %slice_bitcast_fusion.11), channel_id=1, source_target_pairs={{1,0},{3,2},{5,4},{7,6},{9,8},{11,10},{13,12},{15,14},{17,16},{19,... | collective-permute-start | bytes 196616 | tf_op jit(solution)/shard_map/ppermute | solution.py:32
  9.6 0.9 convert_reduce_fusion
  11.7 1.3 select_reduce_fusion.2
  13.7 7.7 %all-to-all-start = ((s32[16,2,1]{1,2,0:T(1,128)}), s32[16,2,1]{1,2,0:T(1,128)}, u32[]{:S(2)}, u32[]{:S(2)}) async-start(s32[16,2,1]{1,2,0:T(1,128)} %bitcast.4), calls=%async_computation | async-start | bytes 16384 | tf_op jit(solution)/shard_map/all_to_all | solution.py:138
  21.4 1.0 convert_bitcast_fusion.1
  22.5 1.6 %convert_bitcast_fusion = bf16[41,256,128]{2,0,1:T(8,128)(2,1)S(1)} fusion(s32[256,128]{1,0:T(8,128)S(1)} %iota_subtract_fusion, bf16[1,41,41]{2,1,0:T(8,128)(2,1)S(1)} %copy-done), kind=kOutput, calls=%fused_computation.83 | convolution fusion | flops 112852992 | bytes 2821410 | tf_op jit(solution)/shard_map/yd,kjd->ykj/dot_general | solution.py:49
  24.1 2.2 %fusion.231 = (bf16[5,256,128]{2,0,1:T(8,128)(2,1)S(1)}, bf16[5,256,128,1]{2,0,1,3:T(8,128)(2,1)}, bf16[5,256,128,1]{2,0,1,3:T(8,128)(2,1)}, bf16[5,256,128,1]{2...) fusion(bf16[41,256,128]{2,0,1:T(8,128)(2,1)S(1)} %convert_bitca, ...), kind=kLoop, calls=%fused_computation.398 | loop fusion | bytes 5242880 | tf_op jit(solution)/shard_map/slice | solution.py:69
  32.7 1.3 %all_to_all.14 = s32[16,2,1]{1,0,2:T(8,128)} reshape(s32[32]{0:T(128)} %get-tuple-element.5) | data formatting | bytes 256 | tf_op jit(solution)/shard_map/all_to_all | solution.py:139
  34.0 1.3 %fusion.232 = (bf16[5,256,128]{2,0,1:T(8,128)(2,1)}, bf16[5,256,128,1]{2,0,1,3:T(8,128)(2,1)}, bf16[5,256,128,1]{2,0,1,3:T(8,128)(2,1)}) fusion(bf16[15,256,128]{2,0,1:T(8,128)(2,1)S(1)} %fusion.4), kind=kLoop, calls=%fused_computation.399 | loop fusion | bytes 1966080 | tf_op jit(solution)/shard_map/slice | solution.py:69
  35.3 6.9 %all-to-all-start.1 = ((s32[16,2,1]{1,2,0:T(1,128)}), s32[16,2,1]{1,2,0:T(1,128)S(1)}, u32[]{:S(2)}, u32[]{:S(2)}) async-start(s32[16,2,1]{1,2,0:T(1,128)} %bitcast.401), calls=%async_computation.1 | async-start | bytes 16384 | tf_op jit(solution)/shard_map/all_to_all | solution.py:139
  42.7 1.4 %reduce.8 = s32[16,2]{1,0:T(8,128)S(1)} reduce(s32[16,2,1]{1,2,0:T(1,128)} %all-to-all-done, s32[]{:T(128)} %broadcast.128), dimensions={2}, to_apply=%all_to_all.13.reduce_sub_computation.3 | reduce | bytes 260 | tf_op jit(solution)/shard_map/all_to_all | solution.py:138
  44.2 5.3 %all-to-all-done.1 = s32[16,2,1]{1,2,0:T(1,128)S(1)} async-done(((s32[16,2,1]{1,2,0:T(1,128)}), s32[16,2,1]{1,2,0:T(1,128)S(1)}, u32[]{:S(2)}, u32[]{:S(2)}) %all-to-all-start.1) | async-done | bytes 160 | tf_op jit(solution)/shard_map/all_to_all | solution.py:139
  51.7 1.1 fusion.210
  53.6 1.0 convolution_convert_fusion
  55.4 4.4 %all-to-all-start.2 = ((bf16[32,24,128]{2,1,0:T(8,128)(2,1)}), bf16[32,24,128]{2,1,0:T(8,128)(2,1)}, u32[]{:S(2)}, u32[]{:S(2)}) async-start(bf16[32,24,128]{2,1,0:T(8,128)(2,1)} %copy.95), calls=%async_computation.2 | async-start | bytes 393216 | tf_op jit(solution)/shard_map/all_to_all | solution.py:137
  59.7 1.3 %fusion.23 = bf16[64,4352]{1,0:T(8,128)(2,1)S(1)} fusion(bf16[20,4096]{1,0:T(8,128)(2,1)} %collective-permute-done.2, bf16[24,4096]{1,0:T(8,128)(2,1)S(1)} %convert_bitcast_fusion.1, bf16[20,4096]{1,0:T(8,128)(2,1)} %collective-permute-done.1), kind=kLoop, calls=%fused_computation.153 | loop fusion | flops 3342336 | bytes 1081344 | tf_op jit(solution)/shard_map/concatenate | solution.py:25
  70.8 1.8 %multiply_reduce_fusion = (f32[]{:T(128)}, f32[24,32,128]{2,1,0:T(8,128)S(1)}) fusion(pred[32,128]{1,0:T(8,128)(4,1)S(1)} %get-tuple-element.55, f32[24,32,128]{2,1,0:T(8,128)S(1)} %convolution_add_fusion, s32[32]{0:T(128)S(1)} %eq.80, bf16[32,24,128]{2,1,0:T(8,128)(2,1)} %all-to-all-done.2), kind=kOutput, calls=%fused_computation.333 | convolution fusion | flops 6685695 | bytes 987268 | tf_op jit(solution)/shard_map/qs,srj->rqj/dot_general | solution.py:142
  72.9 2.3 %collective-permute-start.3 = (bf16[7,4096]{1,0:T(8,128)(2,1)S(1)}, bf16[7,4096]{1,0:T(8,128)(2,1)S(1)}, u32[]{:S(2)}, u32[]{:S(2)}) collective-permute-start(bf16[7,4096]{1,0:T(8,128)(2,1)S(1)} %get-tuple-element.51), channel_id=1, source_target_pairs={{0,1},{2,3},{4,5},{6,7},{8,9},{10,11},{12,13},{14,15},{16,17},{18,... | collective-permute-start | bytes 172040 | tf_op jit(solution)/shard_map/ppermute | solution.py:23
  75.3 1.3 %collective-permute-start.4 = (bf16[7,4096]{1,0:T(8,128)(2,1)S(1)}, bf16[7,4096]{1,0:T(8,128)(2,1)S(1)}, u32[]{:S(2)}, u32[]{:S(2)}) collective-permute-start(bf16[7,4096]{1,0:T(8,128)(2,1)S(1)} %get-tuple-element.52), channel_id=1, source_target_pairs={{1,0},{3,2},{5,4},{7,6},{9,8},{11,10},{13,12},{15,14},{17,16},{19,... | collective-permute-start | bytes 172040 | tf_op jit(solution)/shard_map/ppermute | solution.py:24
  77.4 40.2 %all-reduce.3 = (f32[]{:T(128)}, f32[]{:T(128)}) all-reduce(f32[]{:T(128)} %get-tuple-element.57, f32[]{:T(128)S(6)} %convert_element_type.89), channel_id=1, replica_groups=mesh['ccd'=16,'row'=2] {'ccd','row'}, use_global_device_ids=true, to_apply=%region_5.6 | all-reduce | flops 2 | bytes 16 | tf_op jit(solution)/shard_map/psum | solution.py:87
  (115 shorter events, 27.5 us)
Async XLA Ops:
  0.6 21.8 %copy-start = (bf16[1,41,41]{2,1,0:T(8,128)(2,1)S(1)}, bf16[1,41,41]{2,1,0:T(8,128)(2,1)}, u32[]{:S(2)}) copy-start(bf16[1,41,41]{2,1,0:T(8,128)(2,1)} %param.20) | copy-start | bytes 10090
  2.5 57.3 %collective-permute-start.1 = (bf16[20,4096]{1,0:T(8,128)(2,1)}, bf16[20,4096]{1,0:T(8,128)(2,1)}, u32[]{:S(2)}, u32[]{:S(2)}) collective-permute-start(bf16[20,4096]{1,0:T(8,128)(2,1)} %get-tuple-element.53), channel_id=1, source_target_pairs={{0,1},{2,3},{4,5},{6,7},{8,9},{10,11},{12,13},{14,15},{16,17},{18,... | collective-permute-start | bytes 491528 | tf_op jit(solution)/shard_map/ppermute | solution.py:23
  5.5 54.2 %collective-permute-start.2 = (bf16[20,4096]{1,0:T(8,128)(2,1)}, bf16[20,4096]{1,0:T(8,128)(2,1)}, u32[]{:S(2)}, u32[]{:S(2)}) collective-permute-start(bf16[20,4096]{1,0:T(8,128)(2,1)} %get-tuple-element.54), channel_id=1, source_target_pairs={{1,0},{3,2},{5,4},{7,6},{9,8},{11,10},{13,12},{15,14},{17,16},{19,... | collective-permute-start | bytes 491528 | tf_op jit(solution)/shard_map/ppermute | solution.py:24
  8.3 43.4 %collective-permute-start = (f32[8,2048]{1,0:T(8,128)}, f32[8,2048]{1,0:T(8,128)}, u32[]{:S(2)}, u32[]{:S(2)}) collective-permute-start(f32[8,2048]{1,0:T(8,128)} %slice_bitcast_fusion.11), channel_id=1, source_target_pairs={{1,0},{3,2},{5,4},{7,6},{9,8},{11,10},{13,12},{15,14},{17,16},{19,... | collective-permute-start | bytes 196616 | tf_op jit(solution)/shard_map/ppermute | solution.py:32
  11.2 0.6 copy-start.12
  13.7 21.7 %all-to-all-start = ((s32[16,2,1]{1,2,0:T(1,128)}), s32[16,2,1]{1,2,0:T(1,128)}, u32[]{:S(2)}, u32[]{:S(2)}) async-start(s32[16,2,1]{1,2,0:T(1,128)} %bitcast.4), calls=%async_computation | async-start | bytes 16384 | tf_op jit(solution)/shard_map/all_to_all | solution.py:138
  24.0 3.0 %copy-start.14 = (bf16[1,24]{1,0:T(2,128)(2,1)S(1)}, bf16[1,24]{1,0:T(2,128)(2,1)}, u32[]{:S(2)}) copy-start(bf16[1,24]{1,0:T(2,128)(2,1)} %param.13) | copy-start | bytes 148
  24.1 4.2 %copy-start.13 = (s32[1,16]{1,0:T(1,128)S(1)}, s32[1,16]{1,0:T(1,128)}, u32[]{:S(2)}) copy-start(s32[1,16]{1,0:T(1,128)} %param.16) | copy-start | bytes 196
  24.1 4.8 %copy-start.10 = (bf16[1,2048]{1,0:T(2,128)(2,1)S(1)}, bf16[1,2048]{1,0:T(2,128)(2,1)}, u32[]{:S(2)}) copy-start(bf16[1,2048]{1,0:T(2,128)(2,1)} %param.15) | copy-start | bytes 12292
  24.1 6.0 %copy-start.11 = (bf16[1,15,15]{2,1,0:T(8,128)(2,1)S(1)}, bf16[1,15,15]{2,1,0:T(8,128)(2,1)}, u32[]{:S(2)}) copy-start(bf16[1,15,15]{2,1,0:T(8,128)(2,1)} %param.21) | copy-start | bytes 1354
  30.7 20.9 %copy-start.8 = (f32[1,24,2048]{2,1,0:T(8,128)S(1)}, f32[1,24,2048]{2,1,0:T(8,128)}, u32[]{:S(2)}) copy-start(f32[1,24,2048]{2,1,0:T(8,128)} %param.11) | copy-start | bytes 589828
  35.3 14.2 %all-to-all-start.1 = ((s32[16,2,1]{1,2,0:T(1,128)}), s32[16,2,1]{1,2,0:T(1,128)S(1)}, u32[]{:S(2)}, u32[]{:S(2)}) async-start(s32[16,2,1]{1,2,0:T(1,128)} %bitcast.401), calls=%async_computation.1 | async-start | bytes 16384 | tf_op jit(solution)/shard_map/all_to_all | solution.py:139
  55.4 15.5 %all-to-all-start.2 = ((bf16[32,24,128]{2,1,0:T(8,128)(2,1)}), bf16[32,24,128]{2,1,0:T(8,128)(2,1)}, u32[]{:S(2)}, u32[]{:S(2)}) async-start(bf16[32,24,128]{2,1,0:T(8,128)(2,1)} %copy.95), calls=%async_computation.2 | async-start | bytes 393216 | tf_op jit(solution)/shard_map/all_to_all | solution.py:137
  63.4 1.0 copy-start.4
  63.6 1.5 %copy-start.3 = (bf16[5,256,128,1]{2,0,1,3:T(8,128)(2,1)S(1)}, bf16[5,256,128,1]{2,0,1,3:T(8,128)(2,1)}, u32[]{:S(2)}) copy-start(bf16[5,256,128,1]{2,0,1,3:T(8,128)(2,1)} %get-tuple-element.11) | copy-start | bytes 983044
  65.1 1.0 copy-start.2
  65.8 1.1 copy-start.1
  69.6 0.9 copy-start.9
  72.9 46.7 %collective-permute-start.3 = (bf16[7,4096]{1,0:T(8,128)(2,1)S(1)}, bf16[7,4096]{1,0:T(8,128)(2,1)S(1)}, u32[]{:S(2)}, u32[]{:S(2)}) collective-permute-start(bf16[7,4096]{1,0:T(8,128)(2,1)S(1)} %get-tuple-element.51), channel_id=1, source_target_pairs={{0,1},{2,3},{4,5},{6,7},{8,9},{10,11},{12,13},{14,15},{16,17},{18,... | collective-permute-start | bytes 172040 | tf_op jit(solution)/shard_map/ppermute | solution.py:23
  75.3 44.3 %collective-permute-start.4 = (bf16[7,4096]{1,0:T(8,128)(2,1)S(1)}, bf16[7,4096]{1,0:T(8,128)(2,1)S(1)}, u32[]{:S(2)}, u32[]{:S(2)}) collective-permute-start(bf16[7,4096]{1,0:T(8,128)(2,1)S(1)} %get-tuple-element.52), channel_id=1, source_target_pairs={{1,0},{3,2},{5,4},{7,6},{9,8},{11,10},{13,12},{15,14},{17,16},{19,... | collective-permute-start | bytes 172040 | tf_op jit(solution)/shard_map/ppermute | solution.py:24
  120.9 1.1 copy-start.6
  121.1 1.6 %copy-start.5 = (bf16[5,256,128,1]{2,0,1,3:T(8,128)(2,1)S(1)}, bf16[5,256,128,1]{2,0,1,3:T(8,128)(2,1)}, u32[]{:S(2)}) copy-start(bf16[5,256,128,1]{2,0,1,3:T(8,128)(2,1)} %get-tuple-element.19) | copy-start | bytes 983044
  122.6 1.0 copy-start.7
where the time goes:
time: 127 us; the launch traced here: 126 us
  blocking collectives  40.2 us (32%)
  starting transfers between devices  28.2 us (22%)
  other arithmetic  18.6 us (15%)
  local copies, waits for them, and re-layouts  14.7 us (12%)
  matrix products  12.8 us (10%)
  between operations  6.44 us (5%)
  waiting for transfers between devices  5.34 us (4%)
    psum x1, blocking collectives, noise_totals(): return lax.psum((square_sum, live_count), ('ccd', 'row'))  40.2 us
    dot_general x12, matrix products, banded_filter(): jnp.einsum('rcgk,gkj->rcj', stacked, banded[offset:finish], preferred_ele...  7.79 us
    all_to_all x1, starting transfers between devices, deliver_pieces(): lax.all_to_all(sent_cell, 'ccd', split_axis=0, concat_axis=0, tiled=True)  7.73 us
    all_to_all x1, starting transfers between devices, deliver_pieces(): lax.all_to_all(sent_width, 'ccd', split_axis=0, concat_axis=0, tiled=True)  6.86 us
    ppermute x2, starting transfers between devices, extended_2(): before = lax.ppermute(last, axis, up)  5.4 us
    all_to_all x1, waiting for transfers between devices, deliver_pieces(): lax.all_to_all(sent_width, 'ccd', split_axis=0, concat_axis=0, tiled=True)  5.33 us
    all_to_all x1, starting transfers between devices, deliver_pieces(): lax.all_to_all(outgoing, 'ccd', split_axis=0, concat_axis=0, tiled=True)  4.35 us
    slice x3, local copies, waits for them, and re-layouts, banded_filter(): banded[offset:finish]  4.24 us
  transfers between devices with their start and end apart: 8, of which 1 were waited for; matrix products, arithmetic and copies ran while one was open for 27% of the time, Pallas kernels for 0%

commit v1 on v0

v1 whole, which is shorter than its diff:
```python
import functools

import jax
import jax.numpy as jnp
from jax import lax
from jax.experimental import pallas as pl
from jax.experimental.pallas import tpu as pltpu
from jax.sharding import PartitionSpec as P

PW = 128
PAIR = 2
HALO = 8
SLOT = 32
QUAD = 4
HALF = PW // 2
GROUP = 6
F32 = jnp.float32
BF16 = jnp.bfloat16
MESH = pl.DeviceIdType.MESH


def taps_by_lane(kernel, margin):
    extent = kernel.shape[0]
    b = lax.broadcasted_iota(jnp.int32, (extent, PW), 0)
    lane = lax.broadcasted_iota(jnp.int32, (extent, PW), 1)
    want = margin - b
    want = jnp.where(want < 0, want + PW, want)
    return jnp.dot(kernel, (lane == want).astype(BF16), preferred_element_type=F32)


def build_weights(kernel_ref, taps_ref, taps64_ref, weight_ref):
    extent = kernel_ref.shape[0]
    margin = extent // 2
    taps = taps_by_lane(kernel_ref[...], margin)
    taps_ref[...] = jnp.zeros_like(taps_ref)
    taps64_ref[...] = jnp.zeros_like(taps64_ref)
    taps_ref[8 : 8 + extent, :] = taps
    taps64_ref[8 : 8 + extent, :] = pltpu.roll(taps, HALF, 1)
    lane = lax.broadcasted_iota(jnp.int32, (PW, PW), 1)
    nothing = jnp.zeros((2 * PW, PW), BF16)
    weight_ref[0 : 2 * PW, PW : 2 * PW] = nothing
    weight_ref[(extent + 1) * PW : (extent + 3) * PW, 0:PW] = nothing

    def step(u, carry):
        first = jnp.broadcast_to(taps_ref[pl.ds(u + 8, 1), :], (PW, PW))
        second = jnp.broadcast_to(taps64_ref[pl.ds(u + 7, 1), :], (PW, PW))
        first = pltpu.roll(first, 0, 1, stride=1, stride_axis=0)
        second = pltpu.roll(second, 0, 1, stride=1, stride_axis=0)
        both = jnp.where(lane < HALF, first, second).astype(BF16)
        at = pl.multiple_of(u * PW, PW)
        weight_ref[pl.ds(at, PW), 0:PW] = both
        at = pl.multiple_of((u + 2) * PW, PW)
        weight_ref[pl.ds(at, PW), PW : 2 * PW] = both
        return carry

    lax.fori_loop(0, extent + 1, step, 0)


def build_windows(source_ref, window_ref):
    rows, cells, _ = source_ref.shape

    def step(q, carry):
        x = source_ref[pl.ds(q * QUAD, QUAD)].astype(F32).reshape(QUAD * cells, PW)
        lane = lax.broadcasted_iota(jnp.int32, x.shape, 1)
        cell = lax.broadcasted_iota(jnp.int32, x.shape, 0) % cells
        before = jnp.where(cell == 0, 0.0, pltpu.roll(x, 1, 0))
        after = jnp.where(cell == cells - 1, 0.0, pltpu.roll(x, x.shape[0] - 1, 0))
        even = jnp.where(lane < PW - HALF // 2, x, before)
        odd = pltpu.roll(jnp.where(lane >= HALF // 2, x, after), HALF, 1)
        window_ref[q, :, 0:cells, :] = even.astype(BF16).reshape(QUAD, cells, PW)
        window_ref[q, :, cells : 2 * cells, :] = odd.astype(BF16).reshape(QUAD, cells, PW)
        return carry

    lax.fori_loop(0, rows // QUAD, step, 0)


def run_filter(window_ref, weight_ref, sum_ref, extent, quads):
    reach = extent + QUAD - 1
    blocks = window_ref.shape[2]
    for start in range(0, reach, GROUP):
        stop = min(start + GROUP, reach)
        left = jnp.concatenate(
            [
                window_ref[u // QUAD : u // QUAD + quads, u % QUAD].reshape(quads * blocks, PW)
                for u in range(start, stop)
            ],
            axis=1,
        )
        part = jnp.dot(left, weight_ref[start * PW : stop * PW, :], preferred_element_type=F32)
        if start == 0:
            sum_ref[...] = part
        else:
            sum_ref[...] += part


def filtered_row(sum_ref, row, cells):
    quad, r = divmod(row, QUAD)
    at = quad * 2 * cells
    columns = slice((r // 2) * PW, (r // 2 + 1) * PW)
    even = sum_ref[at : at + cells, columns]
    odd = sum_ref[at + cells : at + 2 * cells, columns]
    lane = lax.broadcasted_iota(jnp.int32, (cells, PW), 1)
    if r % 2 == 0:
        return jnp.where(lane < HALF, even, pltpu.roll(odd, HALF, 1))
    return jnp.where(lane < HALF, pltpu.roll(even, HALF, 1), odd)


def step_kernel(
    n,
    row_shift,
    column_shift,
    piece_width,
    route_tile,
    route_cell,
    exposure,
    row_fraction,
    column_fraction,
    template,
    match_kernel,
    detection_kernel,
    difference,
    significance,
    noise_out,
    extended,
    warped,
    outgoing,
    incoming,
    source,
    window,
    match_weight,
    detect_weight,
    taps,
    taps64,
    total,
    rounded,
    window2,
    partials,
    halo_send,
    halo_recv,
    piece_send,
    piece_recv,
    noise_send,
    noise_recv,
):
    me = lax.axis_index("ccd")
    band = lax.axis_index("row")
    partner = 1 - band
    height, columns = exposure.shape
    pieces = columns // PW
    cells = template.shape[1]
    margin = match_kernel.shape[0] // 2
    margin2 = detection_kernel.shape[0] // 2
    quads = height // QUAD
    everyone = 2 * n

    def peer(index):
        return {
            "ccd": lax.rem(me + lax.rem(index, n), n),
            "row": lax.rem(band + index // n, 2),
        }

    barrier = pltpu.get_barrier_semaphore()

    def greet(index, carry):
        pl.semaphore_signal(barrier, inc=1, device_id=peer(index), device_id_type=MESH)
        return carry

    lax.fori_loop(1, everyone, greet, 0)

    extended[0:height, :] = exposure[...]
    source[margin : margin + height] = template[...]
    outer = jnp.zeros((margin, cells, PW), BF16)
    source[pl.ds(band * (height + margin), margin)] = outer
    rounded[pl.ds(band * (height + margin2), margin2)] = jnp.zeros((margin2, cells, PW), BF16)
    rounded[height + 2 * margin2 :] = jnp.zeros(
        (rounded.shape[0] - height - 2 * margin2, cells, PW), BF16
    )

    pl.semaphore_wait(barrier, everyone - 1)

    exposure_copy = pltpu.make_async_remote_copy(
        src_ref=exposure.at[0:HALO],
        dst_ref=extended.at[height : height + HALO],
        send_sem=halo_send.at[0],
        recv_sem=halo_recv.at[0],
        device_id={"row": partner},
        device_id_type=MESH,
    )
    exposure_copy.start()
    template_copy = pltpu.make_async_remote_copy(
        src_ref=template.at[pl.ds(partner * (height - margin), margin)],
        dst_ref=source.at[pl.ds(band * (height + margin), margin)],
        send_sem=halo_send.at[1],
        recv_sem=halo_recv.at[1],
        device_id={"row": partner},
        device_id_type=MESH,
    )
    template_copy.start()

    build_weights(detection_kernel, taps, taps64, detect_weight)

    exposure_copy.wait()
    below = extended[height : height + HALO, :]
    extended[height : height + HALO, :] = jnp.where(band == 0, below, jnp.zeros_like(below))
    diagonal = lax.broadcasted_iota(jnp.int32, (height, height), 0) == lax.broadcasted_iota(
        jnp.int32, (height, height), 1
    )
    weight = jnp.sum(
        jnp.where(diagonal, jnp.broadcast_to(row_fraction[...].astype(F32), (height, height)), 0.0),
        axis=1,
        keepdims=True,
    )
    shift = row_shift[0]
    slide = column_shift[0]
    lane = lax.broadcasted_iota(jnp.int32, (height, PW), 1)
    all_widths = piece_width[0, 0]
    for p in range(1, pieces):
        all_widths = all_widths + piece_width[0, p]
    meta_row = lax.broadcasted_iota(jnp.int32, (SLOT - height, PW), 0)

    def metadata(cell, width):
        m = jnp.where(meta_row == 0, cell, 0)
        m = jnp.where(meta_row == 1, width, m)
        m = jnp.where(meta_row == 2, all_widths // PW, m)
        m = jnp.where(meta_row == 3, all_widths % PW, m)
        return m.astype(F32)

    rise = height + HALO - shift
    turn1 = lax.rem(PW - slide, PW)
    turn2 = PW - 1 - slide
    after1 = jnp.zeros((height, PW), F32)
    after2 = after1
    warped[pieces] = jnp.concatenate([after1, metadata(-1, 0)], axis=0).astype(BF16)
    for p in reversed(range(pieces)):
        block = slice(p * PW, (p + 1) * PW)
        tall = extended[:, block]
        upper = pltpu.roll(tall, lax.rem(rise, height + HALO), 0)[0:height]
        lower = pltpu.roll(tall, rise - 1, 0)[0:height]
        rows = ((1.0 - weight) * upper + weight * lower).astype(BF16).astype(F32)
        rolled1 = pltpu.roll(rows, turn1, 1)
        rolled2 = pltpu.roll(rows, turn2, 1)
        leftward = jnp.where(lane < PW - slide, rolled1, after1)
        rightward = jnp.where(lane < PW - 1 - slide, rolled2, after2)
        after1, after2 = rolled1, rolled2
        fraction = column_fraction[:, block].astype(F32)
        value = (1.0 - fraction) * leftward + fraction * rightward
        value = jnp.where(lane < piece_width[0, p], value, 0.0)
        warped[p] = jnp.concatenate(
            [value, metadata(route_cell[0, p], piece_width[0, p])], axis=0
        ).astype(BF16)

    def pack(index, carry):
        tile = lax.rem(me + index, n)
        first = pieces
        second = pieces
        for p in reversed(range(pieces)):
            here = route_tile[0, p] == tile
            second = jnp.where(here, first, second)
            first = jnp.where(here, p, first)
        outgoing[index, 0] = warped[first]
        outgoing[index, 1] = warped[second]
        return carry

    lax.fori_loop(0, n, pack, 0)

    def piece_copy(index):
        return pltpu.make_async_remote_copy(
            src_ref=outgoing.at[index],
            dst_ref=incoming.at[index],
            send_sem=piece_send.at[index],
            recv_sem=piece_recv.at[index],
            device_id={"ccd": lax.rem(me + index, n)},
            device_id_type=MESH,
        )

    def send_piece(index, carry):
        piece_copy(index).start()
        return carry

    lax.fori_loop(1, n, send_piece, 0)
    incoming[0] = outgoing[0]

    build_weights(match_kernel, taps, taps64, match_weight)
    template_copy.wait()
    build_windows(source, window)
    run_filter(window, match_weight, total, match_kernel.shape[0], quads)

    def take_piece(index, carry):
        piece_copy(index).wait_recv()
        return carry

    lax.fori_loop(1, n, take_piece, 0)
    chunk = cells // PAIR
    per_vreg = PW // SLOT
    lane_row = lax.broadcasted_iota(jnp.int32, (1, PW), 1)
    cell_of = lax.broadcasted_iota(jnp.int32, (cells, PAIR * chunk * SLOT), 0).astype(F32)
    k_row = lax.broadcasted_iota(jnp.int32, (1, PAIR * chunk * SLOT), 1) % SLOT
    placed_rows = list(range(height)) + [height + 1]
    live_total = jnp.zeros((1, PW), F32)
    placed = None
    for start in range(0, n, chunk):
        meta = [
            incoming[start + s // PAIR, s % PAIR, height : SLOT, :].astype(F32)
            for s in range(PAIR * chunk)
        ]
        for s in range(0, PAIR * chunk, PAIR):
            live_total = live_total + meta[s][2:3] * float(PW) + meta[s][3:4]
        parts = []
        for v in range(PAIR * chunk // per_vreg):
            part = meta[v * per_vreg + per_vreg - 1][0:1]
            for k in reversed(range(per_vreg - 1)):
                part = jnp.where(lane_row < (k + 1) * SLOT, meta[v * per_vreg + k][0:1], part)
            parts.append(part)
        cell_row = jnp.concatenate(parts, axis=1)
        placer = jnp.concatenate(
            [
                jnp.where(jnp.where(k_row == r, cell_row, -1.0) == cell_of, 1.0, 0.0).astype(BF16)
                for r in placed_rows
            ],
            axis=0,
        )
        block = incoming[start : start + chunk].reshape(PAIR * chunk * SLOT, PW)
        got = jnp.dot(placer, block, preferred_element_type=F32)
        placed = got if placed is None else placed + got
    width_of = placed[height * cells : (height + 1) * cells]
    live = lax.broadcasted_iota(jnp.int32, (cells, PW), 1).astype(F32) < width_of
    squares = jnp.zeros((cells, PW), F32)
    for r in range(height):
        d = placed[r * cells : (r + 1) * cells] - filtered_row(total, r, cells)
        d = jnp.where(live, d, 0.0)
        difference[r] = d
        squares = squares + d * d
        rounded[margin2 + r] = d.astype(BF16)
    partials[0] = jnp.sum(squares.reshape(cells // 8, 8, PW), axis=0)

    difference_copy = pltpu.make_async_remote_copy(
        src_ref=rounded.at[pl.ds(margin2 + partner * (height - margin2), margin2)],
        dst_ref=rounded.at[pl.ds(band * (height + margin2), margin2)],
        send_sem=halo_send.at[2],
        recv_sem=halo_recv.at[2],
        device_id={"row": partner},
        device_id_type=MESH,
    )
    difference_copy.start()

    def noise_copy(index):
        return pltpu.make_async_remote_copy(
            src_ref=partials.at[0],
            dst_ref=partials.at[index],
            send_sem=noise_send.at[index],
            recv_sem=noise_recv.at[index],
            device_id=peer(index),
            device_id_type=MESH,
        )

    def send_noise(index, carry):
        noise_copy(index).start()
        return carry

    lax.fori_loop(1, everyone, send_noise, 0)

    difference_copy.wait()
    build_windows(rounded, window2)
    run_filter(window2, detect_weight, total, detection_kernel.shape[0], quads)

    def take_noise(index, carry):
        noise_copy(index).wait()
        return carry

    lax.fori_loop(1, everyone, take_noise, 0)

    def end_piece(index, carry):
        piece_copy(index).wait_send()
        return carry

    lax.fori_loop(1, n, end_piece, 0)

    squares = jnp.sum(partials[...], axis=0)
    square_sum = jnp.sum(jnp.sum(squares, axis=0, keepdims=True), axis=1, keepdims=True)
    live_count = live_total[:, 0:1] * float(2 * height)
    noise = square_sum / live_count
    detect = detection_kernel[...].astype(F32)
    norm = jnp.sum(jnp.sum(detect * detect, axis=0, keepdims=True), axis=1, keepdims=True)
    scale = 1.0 / jnp.sqrt(1.0 + noise * norm)
    scale = jnp.broadcast_to(scale, (cells, PW))
    for r in range(height):
        significance[r] = filtered_row(total, r, cells) * scale
    noise_out[...] = jnp.broadcast_to(noise, noise_out.shape)


def on_device(
    n,
    exposure,
    row_shift,
    row_fraction,
    column_shift,
    column_fraction,
    piece_width,
    route_tile,
    route_cell,
    template,
    match_kernel,
    detection_kernel,
):
    height, columns = exposure.shape[1:]
    pieces = columns // PW
    cells = template.shape[2] // PW
    extent = match_kernel.shape[1]
    extent2 = detection_kernel.shape[1]
    rows = height + 2 * (extent // 2)
    rows2 = -(-(height + 2 * (extent2 // 2)) // QUAD) * QUAD
    smem = pl.BlockSpec(memory_space=pltpu.SMEM)
    vmem = pl.BlockSpec(memory_space=pltpu.VMEM)
    tiles = template[0].astype(BF16).reshape(height, cells, PW)
    difference, significance, noise = pl.pallas_call(
        functools.partial(step_kernel, n),
        out_shape=(
            jax.ShapeDtypeStruct((height, cells, PW), F32),
            jax.ShapeDtypeStruct((height, cells, PW), F32),
            jax.ShapeDtypeStruct((8, PW), F32),
        ),
        in_specs=[smem] * 5 + [vmem] * 6,
        out_specs=(vmem, vmem, vmem),
        scratch_shapes=[
            pltpu.VMEM((height + HALO, columns), F32),
            pltpu.VMEM((pieces + 1, SLOT, PW), BF16),
            pltpu.VMEM((n, PAIR, SLOT, PW), BF16),
            pltpu.VMEM((n, PAIR, SLOT, PW), BF16),
            pltpu.VMEM((rows, cells, PW), BF16),
            pltpu.VMEM((rows // QUAD, QUAD, 2 * cells, PW), BF16),
            pltpu.VMEM(((extent + QUAD - 1) * PW, 2 * PW), BF16),
            pltpu.VMEM(((extent2 + QUAD - 1) * PW, 2 * PW), BF16),
            pltpu.VMEM((extent + 15, PW), F32),
            pltpu.VMEM((extent + 15, PW), F32),
            pltpu.VMEM((height // QUAD * 2 * cells, 2 * PW), F32),
            pltpu.VMEM((rows2, cells, PW), BF16),
            pltpu.VMEM((rows2 // QUAD, QUAD, 2 * cells, PW), BF16),
            pltpu.VMEM((2 * n, 8, PW), F32),
            pltpu.SemaphoreType.DMA((3,)),
            pltpu.SemaphoreType.DMA((3,)),
            pltpu.SemaphoreType.DMA((n,)),
            pltpu.SemaphoreType.DMA((n,)),
            pltpu.SemaphoreType.DMA((2 * n,)),
            pltpu.SemaphoreType.DMA((2 * n,)),
        ],
        compiler_params=pltpu.CompilerParams(
            collective_id=0, has_side_effects=True, vmem_limit_bytes=40 * 2**20
        ),
    )(
        row_shift,
        column_shift,
        piece_width,
        route_tile,
        route_cell,
        exposure[0],
        row_fraction,
        column_fraction,
        tiles,
        match_kernel[0],
        detection_kernel[0],
    )
    shape = (1, height, cells * PW)
    return (difference.reshape(shape), significance.reshape(shape), noise[0, 0])


def solution(mesh):
    assert mesh.shape["row"] == 2
    return jax.shard_map(
        functools.partial(on_device, mesh.shape["ccd"]),
        mesh=mesh,
        in_specs=(
            P("ccd", "row", None),
            P("ccd"),
            P("ccd", "row"),
            P("ccd"),
            P("ccd", None),
            P("ccd", None),
            P("ccd", None),
            P("ccd", None),
            P("ccd", "row", None),
            P("ccd", None, None),
            P("ccd", None, None),
        ),
        out_specs=(P("ccd", "row", None), P("ccd", "row", None), P()),
        check_vma=False,
    )
```

time: 127 us -> 32 us (0.25)
  blocking collectives: 40.2 us -> 0 us
  starting transfers between devices: 28.2 us -> 0 us
  Pallas kernels: 0 us -> 25.7 us
  other arithmetic: 18.6 us -> 1.02 us
  matrix products: 12.8 us -> 0 us
  local copies, waits for them, and re-layouts: 14.7 us -> 3.02 us
  waiting for transfers between devices: 5.34 us -> 0 us
  between operations: 6.44 us -> 2.03 us
    psum x1 -> x0, blocking collectives: 40.2 us -> none  [noise_totals(): return lax.psum((square_sum, live_count), ('ccd', 'row'))]
    pallas_call x0 -> x1, Pallas kernels: none -> 25.7 us  [on_device(): pl.pallas_call(functools.partial(step_kernel, n), out_shape=(jax.ShapeDty...]
    all_to_all x3 -> x0, starting transfers between devices: 18.9 us -> none  [the longest x1 7.73 us: deliver_pieces(): lax.all_to_all(sent_cell, 'ccd', split_axis=0, concat_axis=0, tiled=True)]
    dot_general x16 -> x0, matrix products: 12.8 us -> none  [the longest x12 7.79 us: banded_filter(): jnp.einsum('rcgk,gkj->rcj', stacked, banded[offset:finish], preferred_ele...]
    ppermute x5 -> x0, starting transfers between devices: 9.25 us -> none  [the longest x2 5.4 us: extended_2(): before = lax.ppermute(last, axis, up)]
    slice x8 -> x1, local copies, waits for them, and re-layouts: 6.9 us -> 0.51 us  [on_device(): return (difference.reshape(shape), significance.reshape(shape), noise[0, 0])]
    all_to_all x3 -> x0, waiting for transfers between devices: 5.33 us -> none  [the longest x1 5.33 us: deliver_pieces(): lax.all_to_all(sent_width, 'ccd', split_axis=0, concat_axis=0, tiled=True)]
    convert_element_type x6 -> x0, other arithmetic: 4.52 us -> none  [the longest x2 2.04 us: match_template(): rounded = template[0].astype(jnp.bfloat16)]
  transfers between devices with their start and end apart: 8 -> 0, of which waited for: 1 -> 0; matrix products, arithmetic and copies ran while one was open for 27% -> 0% of each run, Pallas kernels for 0% -> 0%
where the time goes in v1:
time: 32 us; the launch traced here: 31.8 us
  Pallas kernels  25.7 us (80%)
  local copies, waits for them, and re-layouts  3.02 us (9%)
  between operations  2.03 us (6%)
  other arithmetic  1.02 us (3%)
    pallas_call x1, Pallas kernels, on_device(): pl.pallas_call(functools.partial(step_kernel, n), out_shape=(jax.ShapeDty...  25.7 us
    reshape x2, local copies, waits for them, and re-layouts, on_device(): return (difference.reshape(shape), significance.reshape(shape), noise[0, 0])  1.64 us
    unnamed x1, other arithmetic  1.02 us
    unnamed x17, local copies, waits for them, and re-layouts  0.87 us

profile of v1, /device:TPU:0, one launch (start us, length us, event | category | flops | bytes accessed | tf_op | source)
XLA Modules:
  0.0 31.8 jit_solution(10843067840244688329)
XLA Ops:
  1.9 1.0 %convert_bitcast_fusion = bf16[3,8,32,128]{3,1,2,0:T(8,128)(2,1)S(1)} fusion(f32[1,24,4096]{2,1,0:T(8,128)} %param.19), kind=kLoop, calls=%fused_computation | loop fusion | flops 98304 | bytes 589824
  2.9 0.0 copy-start
  3.0 0.0 copy-start.1
  3.0 0.0 copy-start.2
  3.0 0.0 copy-start.3
  3.0 0.0 copy-start.7
  3.0 0.0 copy-start.4
  3.1 0.0 copy-start.5
  3.1 0.0 copy-start.6
  3.1 0.8 %copy-done = f32[1,24,2048]{2,1,0:T(8,128)S(1)} copy-done((f32[1,24,2048]{2,1,0:T(8,128)S(1)}, f32[1,24,2048]{2,1,0:T(8,128)}, u32[]{:S(2)}) %copy-start) | copy-done | bytes 196632
  3.9 0.0 copy-done.1
  3.9 0.0 copy-done.2
  3.9 0.0 copy-done.3
  3.9 0.0 copy-done.7
  3.9 0.0 copy-done.4
  3.9 0.0 copy-done.5
  3.9 0.0 copy-done.6
  3.9 25.7 %shard_map.130 = (f32[24,32,128]{2,1,0:T(8,128)S(1)}, f32[24,32,128]{2,1,0:T(8,128)S(1)}, f32[8,128]{1,0:T(8,128)S(1)}) custom-call(s32[1]{0:T(128)S(6)} %copy.15.row_shift, s32[1]{0:T(128)S(6)} %copy.16.column_shift, s32[1,16]{1,0:T(1,128)S(1)} %copy-done.4, s32[1,16]{1,0:T(1,128)S(1)} %copy-done.5, s32[1,16]{1,0:T(1,128)S(1)} %copy-done.6, ...), custom_call_target="tpu_custom_call" | custom-call | tf_op jit(solution)/shard_map/pallas_call | solution.py:415
  29.6 0.5 %slice.3 = f32[1,1]{1,0:T(1,128)} slice(f32[8,128]{1,0:T(8,128)S(1)} %get-tuple-element.8), slice={[0:1], [0:1]} | slice | bytes 8 | tf_op jit(solution)/shard_map/slice | solution.py:463
  30.2 0.8 %reshape.15 = f32[1,24,4096]{2,1,0:T(8,128)} reshape(f32[24,32,128]{2,1,0:T(8,128)S(1)} %get-tuple-element.6) | data formatting | bytes 786432 | tf_op jit(solution)/shard_map/reshape | solution.py:463
  31.0 0.8 %reshape.16 = f32[1,24,4096]{2,1,0:T(8,128)} reshape(f32[24,32,128]{2,1,0:T(8,128)S(1)} %get-tuple-element.7) | data formatting | bytes 786432 | tf_op jit(solution)/shard_map/reshape | solution.py:463
  (1 shorter events, 0.0 us)
Async XLA Ops:
  2.9 0.9 %copy-start = (f32[1,24,2048]{2,1,0:T(8,128)S(1)}, f32[1,24,2048]{2,1,0:T(8,128)}, u32[]{:S(2)}) copy-start(f32[1,24,2048]{2,1,0:T(8,128)} %param.11) | copy-start | bytes 589828
  3.0 0.9 %copy-start.1 = (bf16[1,41,41]{2,1,0:T(8,128)(2,1)S(1)}, bf16[1,41,41]{2,1,0:T(8,128)(2,1)}, u32[]{:S(2)}) copy-start(bf16[1,41,41]{2,1,0:T(8,128)(2,1)} %param.20) | copy-start | bytes 10090
  3.0 0.9 %copy-start.2 = (bf16[1,2048]{1,0:T(2,128)(2,1)S(1)}, bf16[1,2048]{1,0:T(2,128)(2,1)}, u32[]{:S(2)}) copy-start(bf16[1,2048]{1,0:T(2,128)(2,1)} %column_fraction.1) | copy-start | bytes 12292
  3.0 0.9 %copy-start.3 = (bf16[1,15,15]{2,1,0:T(8,128)(2,1)S(1)}, bf16[1,15,15]{2,1,0:T(8,128)(2,1)}, u32[]{:S(2)}) copy-start(bf16[1,15,15]{2,1,0:T(8,128)(2,1)} %param.21) | copy-start | bytes 1354
  3.0 0.9 %copy-start.7 = (bf16[1,24]{1,0:T(2,128)(2,1)S(1)}, bf16[1,24]{1,0:T(2,128)(2,1)}, u32[]{:S(2)}) copy-start(bf16[1,24]{1,0:T(2,128)(2,1)} %row_fraction.1) | copy-start | bytes 148
  3.0 0.8 %copy-start.4 = (s32[1,16]{1,0:T(1,128)S(1)}, s32[1,16]{1,0:T(1,128)}, u32[]{:S(2)}) copy-start(s32[1,16]{1,0:T(1,128)} %piece_width.1) | copy-start | bytes 196
  3.1 0.8 %copy-start.5 = (s32[1,16]{1,0:T(1,128)S(1)}, s32[1,16]{1,0:T(1,128)}, u32[]{:S(2)}) copy-start(s32[1,16]{1,0:T(1,128)} %route_tile.1) | copy-start | bytes 196
  3.1 0.8 %copy-start.6 = (s32[1,16]{1,0:T(1,128)S(1)}, s32[1,16]{1,0:T(1,128)}, u32[]{:S(2)}) copy-start(s32[1,16]{1,0:T(1,128)} %route_cell.1) | copy-start | bytes 196

commit v2 on v1

--- a/solution.py
+++ b/solution.py
@@ -56,10 +56,11 @@
     lax.fori_loop(0, extent + 1, step, 0)
 
 
-def build_windows(source_ref, window_ref):
+def build_windows(source_ref, window_ref, first, count):
     rows, cells, _ = source_ref.shape
 
-    def step(q, carry):
+    def step(index, carry):
+        q = first + index
         x = source_ref[pl.ds(q * QUAD, QUAD)].astype(F32).reshape(QUAD * cells, PW)
         lane = lax.broadcasted_iota(jnp.int32, x.shape, 1)
         cell = lax.broadcasted_iota(jnp.int32, x.shape, 0) % cells
@@ -71,17 +72,17 @@
         window_ref[q, :, cells : 2 * cells, :] = odd.astype(BF16).reshape(QUAD, cells, PW)
         return carry
 
-    lax.fori_loop(0, rows // QUAD, step, 0)
-
-
-def run_filter(window_ref, weight_ref, sum_ref, extent, quads):
+    lax.fori_loop(0, count, step, 0)
+
+
+def run_filter(window_ref, weight_ref, sum_ref, extent, quads, skip):
     reach = extent + QUAD - 1
     blocks = window_ref.shape[2]
     for start in range(0, reach, GROUP):
         stop = min(start + GROUP, reach)
         left = jnp.concatenate(
             [
-                window_ref[u // QUAD : u // QUAD + quads, u % QUAD].reshape(quads * blocks, PW)
+                window_ref[(u + skip) // QUAD : (u + skip) // QUAD + quads, (u + skip) % QUAD].reshape(quads * blocks, PW)
                 for u in range(start, stop)
             ],
             axis=1,
@@ -125,6 +126,7 @@
     warped,
     outgoing,
     incoming,
+    tiles,
     source,
     window,
     match_weight,
@@ -147,17 +149,25 @@
     partner = 1 - band
     height, columns = exposure.shape
     pieces = columns // PW
-    cells = template.shape[1]
+    cells = template.shape[0] // height
     margin = match_kernel.shape[0] // 2
     margin2 = detection_kernel.shape[0] // 2
     quads = height // QUAD
     everyone = 2 * n
+    rows2 = rounded.shape[0]
+    lead = rows2 // 2 - height // 2
 
     def peer(index):
+        other = index >= n
+        at = me + jnp.where(other, index - n, index)
         return {
-            "ccd": lax.rem(me + lax.rem(index, n), n),
-            "row": lax.rem(band + index // n, 2),
+            "ccd": jnp.where(at >= n, at - n, at),
+            "row": jnp.where(other, partner, band),
         }
+
+    def along(index):
+        at = me + index
+        return jnp.where(at >= n, at - n, at)
 
     barrier = pltpu.get_barrier_semaphore()
 
@@ -168,13 +178,17 @@
     lax.fori_loop(1, everyone, greet, 0)
 
     extended[0:height, :] = exposure[...]
-    source[margin : margin + height] = template[...]
     outer = jnp.zeros((margin, cells, PW), BF16)
     source[pl.ds(band * (height + margin), margin)] = outer
-    rounded[pl.ds(band * (height + margin2), margin2)] = jnp.zeros((margin2, cells, PW), BF16)
-    rounded[height + 2 * margin2 :] = jnp.zeros(
-        (rounded.shape[0] - height - 2 * margin2, cells, PW), BF16
-    )
+    for r in range(height):
+        tiles[r] = template[pl.ds(r // 8 * cells * 8 + r % 8, cells, stride=8), :].astype(BF16)
+    source[margin : margin + height] = tiles[...]
+    for q in (0, 1, rows2 // QUAD - 2, rows2 // QUAD - 1):
+        rounded[q * QUAD : (q + 1) * QUAD] = jnp.zeros((QUAD, cells, PW), BF16)
+    build_weights(detection_kernel, taps, taps64, detect_weight)
+    build_weights(match_kernel, taps, taps64, match_weight)
+    build_windows(source, window, margin // QUAD, quads)
+    build_windows(source, window, band * ((height + margin) // QUAD), margin // QUAD)
 
     pl.semaphore_wait(barrier, everyone - 1)
 
@@ -188,7 +202,7 @@
     )
     exposure_copy.start()
     template_copy = pltpu.make_async_remote_copy(
-        src_ref=template.at[pl.ds(partner * (height - margin), margin)],
+        src_ref=tiles.at[pl.ds(partner * (height - margin), margin)],
         dst_ref=source.at[pl.ds(band * (height + margin), margin)],
         send_sem=halo_send.at[1],
         recv_sem=halo_recv.at[1],
@@ -196,8 +210,6 @@
         device_id_type=MESH,
     )
     template_copy.start()
-
-    build_weights(detection_kernel, taps, taps64, detect_weight)
 
     exposure_copy.wait()
     below = extended[height : height + HALO, :]
@@ -250,7 +262,7 @@
         ).astype(BF16)
 
     def pack(index, carry):
-        tile = lax.rem(me + index, n)
+        tile = along(index)
         first = pieces
         second = pieces
         for p in reversed(range(pieces)):
@@ -269,7 +281,7 @@
             dst_ref=incoming.at[index],
             send_sem=piece_send.at[index],
             recv_sem=piece_recv.at[index],
-            device_id={"ccd": lax.rem(me + index, n)},
+            device_id={"ccd": along(index)},
             device_id_type=MESH,
         )
 
@@ -280,10 +292,9 @@
     lax.fori_loop(1, n, send_piece, 0)
     incoming[0] = outgoing[0]
 
-    build_weights(match_kernel, taps, taps64, match_weight)
     template_copy.wait()
-    build_windows(source, window)
-    run_filter(window, match_weight, total, match_kernel.shape[0], quads)
+    build_windows(source, window, partner * ((height + margin) // QUAD), margin // QUAD)
+    run_filter(window, match_weight, total, match_kernel.shape[0], quads, 0)
 
     def take_piece(index, carry):
         piece_copy(index).wait_recv()
@@ -328,14 +339,14 @@
     for r in range(height):
         d = placed[r * cells : (r + 1) * cells] - filtered_row(total, r, cells)
         d = jnp.where(live, d, 0.0)
-        difference[r] = d
+        difference[pl.ds(r // 8 * cells * 8 + r % 8, cells, stride=8), :] = d
         squares = squares + d * d
-        rounded[margin2 + r] = d.astype(BF16)
+        rounded[lead + r] = d.astype(BF16)
     partials[0] = jnp.sum(squares.reshape(cells // 8, 8, PW), axis=0)
 
     difference_copy = pltpu.make_async_remote_copy(
-        src_ref=rounded.at[pl.ds(margin2 + partner * (height - margin2), margin2)],
-        dst_ref=rounded.at[pl.ds(band * (height + margin2), margin2)],
+        src_ref=rounded.at[pl.ds(lead + partner * (height - margin2), margin2)],
+        dst_ref=rounded.at[pl.ds(lead - margin2 + band * (height + margin2), margin2)],
         send_sem=halo_send.at[2],
         recv_sem=halo_recv.at[2],
         device_id={"row": partner},
@@ -359,9 +370,11 @@
 
     lax.fori_loop(1, everyone, send_noise, 0)
 
+    build_windows(rounded, window2, lead // QUAD, quads)
+    build_windows(rounded, window2, band * ((height + lead) // QUAD), lead // QUAD)
     difference_copy.wait()
-    build_windows(rounded, window2)
-    run_filter(window2, detect_weight, total, detection_kernel.shape[0], quads)
+    build_windows(rounded, window2, partner * ((height + lead) // QUAD), lead // QUAD)
+    run_filter(window2, detect_weight, total, detection_kernel.shape[0], quads, lead - margin2)
 
     def take_noise(index, carry):
         noise_copy(index).wait()
@@ -384,8 +397,10 @@
     scale = 1.0 / jnp.sqrt(1.0 + noise * norm)
     scale = jnp.broadcast_to(scale, (cells, PW))
     for r in range(height):
-        significance[r] = filtered_row(total, r, cells) * scale
-    noise_out[...] = jnp.broadcast_to(noise, noise_out.shape)
+        significance[pl.ds(r // 8 * cells * 8 + r % 8, cells, stride=8), :] = (
+            filtered_row(total, r, cells) * scale
+        )
+    noise_out[...] = noise
 
 
 def on_device(
@@ -408,16 +423,16 @@
     extent = match_kernel.shape[1]
     extent2 = detection_kernel.shape[1]
     rows = height + 2 * (extent // 2)
-    rows2 = -(-(height + 2 * (extent2 // 2)) // QUAD) * QUAD
+    rows2 = height + 2 * QUAD * -(-(extent2 // 2) // QUAD)
     smem = pl.BlockSpec(memory_space=pltpu.SMEM)
     vmem = pl.BlockSpec(memory_space=pltpu.VMEM)
-    tiles = template[0].astype(BF16).reshape(height, cells, PW)
+    tiles = template.reshape(height // 8, 8, cells, PW).transpose(0, 2, 1, 3).reshape(height * cells, PW)
     difference, significance, noise = pl.pallas_call(
         functools.partial(step_kernel, n),
         out_shape=(
-            jax.ShapeDtypeStruct((height, cells, PW), F32),
-            jax.ShapeDtypeStruct((height, cells, PW), F32),
-            jax.ShapeDtypeStruct((8, PW), F32),
+            jax.ShapeDtypeStruct((height * cells, PW), F32),
+            jax.ShapeDtypeStruct((height * cells, PW), F32),
+            jax.ShapeDtypeStruct((1, 1), F32),
         ),
         in_specs=[smem] * 5 + [vmem] * 6,
         out_specs=(vmem, vmem, vmem),
@@ -426,6 +441,7 @@
             pltpu.VMEM((pieces + 1, SLOT, PW), BF16),
             pltpu.VMEM((n, PAIR, SLOT, PW), BF16),
             pltpu.VMEM((n, PAIR, SLOT, PW), BF16),
+            pltpu.VMEM((height, cells, PW), BF16),
             pltpu.VMEM((rows, cells, PW), BF16),
             pltpu.VMEM((rows // QUAD, QUAD, 2 * cells, PW), BF16),
             pltpu.VMEM(((extent + QUAD - 1) * PW, 2 * PW), BF16),
@@ -459,8 +475,12 @@
         match_kernel[0],
         detection_kernel[0],
     )
-    shape = (1, height, cells * PW)
-    return (difference.reshape(shape), significance.reshape(shape), noise[0, 0])
+
+    def as_rows(x):
+        x = x.reshape(height // 8, cells, 8, PW).transpose(0, 2, 1, 3)
+        return x.reshape(1, height, cells * PW)
+
+    return (as_rows(difference), as_rows(significance), noise.reshape(()))
 
 
 def solution(mesh):

time: 32 us -> 37.7 us (1.18)
  local copies, waits for them, and re-layouts: 3.02 us -> 5.47 us
  Pallas kernels: 25.7 us -> 28.1 us
  between operations: 2.03 us -> 3.76 us
  other arithmetic: 1.02 us -> 0 us
    unnamed x17 -> x20, local copies, waits for them, and re-layouts: 0.87 us -> 5.47 us
    pallas_call x1, Pallas kernels: 25.7 us -> 28.1 us  [on_device(): pl.pallas_call(functools.partial(step_kernel, n), out_shape=(jax.ShapeDty...]
    reshape x2 -> x0, local copies, waits for them, and re-layouts: 1.64 us -> none  [on_device(): return (difference.reshape(shape), significance.reshape(shape), noise[0, 0])]
    unnamed x1 -> x0, other arithmetic: 1.02 us -> none
    slice x1 -> x0, local copies, waits for them, and re-layouts: 0.51 us -> none  [on_device(): return (difference.reshape(shape), significance.reshape(shape), noise[0, 0])]
where the time goes in v2:
time: 37.7 us; the launch traced here: 37.3 us
  Pallas kernels  28.1 us (75%)
  local copies, waits for them, and re-layouts  5.47 us (15%)
  between operations  3.76 us (10%)
    pallas_call x1, Pallas kernels, on_device(): pl.pallas_call(functools.partial(step_kernel, n), out_shape=(jax.ShapeDty...  28.1 us
    unnamed x20, local copies, waits for them, and re-layouts  5.47 us

profile of v2, /device:TPU:0, one launch (start us, length us, event | category | flops | bytes accessed | tf_op | source)
XLA Modules:
  0.0 37.3 jit_solution(1263337756050264712)
XLA Ops:
  0.6 0.0 copy-start.3
  1.9 0.0 copy-start.8
  2.0 0.0 copy-start.5
  2.0 0.0 copy-start.6
  2.0 0.0 copy-start.7
  2.0 0.0 copy-done.3
  2.0 0.6 %copy-done.8 = bf16[1,24]{1,0:T(2,128)(2,1)S(1)} copy-done((bf16[1,24]{1,0:T(2,128)(2,1)S(1)}, bf16[1,24]{1,0:T(2,128)(2,1)}, u32[]{:S(2)}) %copy-start.8) | copy-done | bytes 72
  2.6 0.0 copy-done.5
  2.6 0.0 copy-done.6
  2.6 0.0 copy-done.7
  2.7 0.0 copy-start
  2.7 1.0 %copy-done = f32[1,24,4096]{2,1,0:T(8,128)S(1)} copy-done((f32[1,24,4096]{2,1,0:T(8,128)S(1)}, f32[1,24,4096]{2,1,0:T(8,128)}, u32[]{:S(2)}) %copy-start) | copy-done | bytes 393240
  3.6 0.0 copy-start.1
  3.6 0.9 %copy-done.1 = f32[1,24,2048]{2,1,0:T(8,128)S(1)} copy-done((f32[1,24,2048]{2,1,0:T(8,128)S(1)}, f32[1,24,2048]{2,1,0:T(8,128)}, u32[]{:S(2)}) %copy-start.1) | copy-done | bytes 196632
  4.6 0.0 copy-start.2
  4.6 0.7 %copy-done.2 = bf16[1,41,41]{2,1,0:T(8,128)(2,1)S(1)} copy-done((bf16[1,41,41]{2,1,0:T(8,128)(2,1)S(1)}, bf16[1,41,41]{2,1,0:T(8,128)(2,1)}, u32[]{:S(2)}) %copy-start.2) | copy-done | bytes 3386
  5.3 0.0 copy-start.4
  5.3 0.7 %copy-done.4 = bf16[1,15,15]{2,1,0:T(8,128)(2,1)S(1)} copy-done((bf16[1,15,15]{2,1,0:T(8,128)(2,1)S(1)}, bf16[1,15,15]{2,1,0:T(8,128)(2,1)}, u32[]{:S(2)}) %copy-start.4) | copy-done | bytes 474
  6.0 28.1 %shard_map.130 = (f32[768,128]{1,0:T(8,128)S(1)}, f32[768,128]{1,0:T(8,128)S(1)}, f32[1,1]{1,0:T(1,128)}) custom-call(s32[1]{0:T(128)S(6)} %copy.17.row_shift, s32[1]{0:T(128)S(6)} %copy.18.column_shift, s32[1,16]{1,0:T(1,128)S(1)} %copy-done.5, s32[1,16]{1,0:T(1,128)S(1)} %copy-done.6, s32[1,16]{1,0:T(1,128)S(1)} %copy-done.7, f32[24,2048]{1,0:T(8,128)S(1)} %bitcast.22, ...), custom_call_target="tpu_custom_call" | custom-call | tf_op jit(solution)/shard_map/pallas_call | solution.py:430
  34.1 0.7 %copy.19 = f32[1,24,4096]{2,1,0:T(8,128)} copy(f32[1,24,4096]{2,1,0:T(8,128)S(1)} %bitcast.21) | data formatting | bytes 786432
  34.8 0.7 %copy.20 = f32[1,24,4096]{2,1,0:T(8,128)} copy(f32[1,24,4096]{2,1,0:T(8,128)S(1)} %bitcast.20) | data formatting | bytes 786432
Async XLA Ops:
  0.6 1.4 %copy-start.3 = (bf16[1,2048]{1,0:T(2,128)(2,1)S(1)}, bf16[1,2048]{1,0:T(2,128)(2,1)}, u32[]{:S(2)}) copy-start(bf16[1,2048]{1,0:T(2,128)(2,1)} %column_fraction.1) | copy-start | bytes 12292
  1.9 0.7 %copy-start.8 = (bf16[1,24]{1,0:T(2,128)(2,1)S(1)}, bf16[1,24]{1,0:T(2,128)(2,1)}, u32[]{:S(2)}) copy-start(bf16[1,24]{1,0:T(2,128)(2,1)} %row_fraction.1) | copy-start | bytes 148
  2.0 0.7 %copy-start.5 = (s32[1,16]{1,0:T(1,128)S(1)}, s32[1,16]{1,0:T(1,128)}, u32[]{:S(2)}) copy-start(s32[1,16]{1,0:T(1,128)} %piece_width.1) | copy-start | bytes 196
  2.0 0.7 %copy-start.6 = (s32[1,16]{1,0:T(1,128)S(1)}, s32[1,16]{1,0:T(1,128)}, u32[]{:S(2)}) copy-start(s32[1,16]{1,0:T(1,128)} %route_tile.1) | copy-start | bytes 196
  2.0 0.7 %copy-start.7 = (s32[1,16]{1,0:T(1,128)S(1)}, s32[1,16]{1,0:T(1,128)}, u32[]{:S(2)}) copy-start(s32[1,16]{1,0:T(1,128)} %route_cell.1) | copy-start | bytes 196
  2.7 1.0 %copy-start = (f32[1,24,4096]{2,1,0:T(8,128)S(1)}, f32[1,24,4096]{2,1,0:T(8,128)}, u32[]{:S(2)}) copy-start(f32[1,24,4096]{2,1,0:T(8,128)} %param.19) | copy-start | bytes 1179652
  3.6 0.9 %copy-start.1 = (f32[1,24,2048]{2,1,0:T(8,128)S(1)}, f32[1,24,2048]{2,1,0:T(8,128)}, u32[]{:S(2)}) copy-start(f32[1,24,2048]{2,1,0:T(8,128)} %param.11) | copy-start | bytes 589828
  4.6 0.7 %copy-start.2 = (bf16[1,41,41]{2,1,0:T(8,128)(2,1)S(1)}, bf16[1,41,41]{2,1,0:T(8,128)(2,1)}, u32[]{:S(2)}) copy-start(bf16[1,41,41]{2,1,0:T(8,128)(2,1)} %param.20) | copy-start | bytes 10090
  5.3 0.7 %copy-start.4 = (bf16[1,15,15]{2,1,0:T(8,128)(2,1)S(1)}, bf16[1,15,15]{2,1,0:T(8,128)(2,1)}, u32[]{:S(2)}) copy-start(bf16[1,15,15]{2,1,0:T(8,128)(2,1)} %param.21) | copy-start | bytes 1354

commit v3 on v2

--- a/solution.py
+++ b/solution.py
@@ -28,32 +28,37 @@
     return jnp.dot(kernel, (lane == want).astype(BF16), preferred_element_type=F32)
 
 
-def build_weights(kernel_ref, taps_ref, taps64_ref, weight_ref):
+def build_weights(kernel_ref, taps_ref, weight_ref):
     extent = kernel_ref.shape[0]
     margin = extent // 2
-    taps = taps_by_lane(kernel_ref[...], margin)
     taps_ref[...] = jnp.zeros_like(taps_ref)
-    taps64_ref[...] = jnp.zeros_like(taps64_ref)
-    taps_ref[8 : 8 + extent, :] = taps
-    taps64_ref[8 : 8 + extent, :] = pltpu.roll(taps, HALF, 1)
+    taps_ref[8 : 8 + extent, :] = taps_by_lane(kernel_ref[...], margin)
     lane = lax.broadcasted_iota(jnp.int32, (PW, PW), 1)
     nothing = jnp.zeros((2 * PW, PW), BF16)
     weight_ref[0 : 2 * PW, PW : 2 * PW] = nothing
     weight_ref[(extent + 1) * PW : (extent + 3) * PW, 0:PW] = nothing
 
-    def step(u, carry):
-        first = jnp.broadcast_to(taps_ref[pl.ds(u + 8, 1), :], (PW, PW))
-        second = jnp.broadcast_to(taps64_ref[pl.ds(u + 7, 1), :], (PW, PW))
-        first = pltpu.roll(first, 0, 1, stride=1, stride_axis=0)
-        second = pltpu.roll(second, 0, 1, stride=1, stride_axis=0)
+    def circulant(u):
+        row = jnp.broadcast_to(taps_ref[pl.ds(u + 8, 1), :], (PW, PW))
+        return pltpu.roll(row, 0, 1, stride=1, stride_axis=0)
+
+    def place(u, first, second):
+        second = jnp.concatenate([second[HALF:], second[:HALF]], axis=0)
         both = jnp.where(lane < HALF, first, second).astype(BF16)
         at = pl.multiple_of(u * PW, PW)
         weight_ref[pl.ds(at, PW), 0:PW] = both
         at = pl.multiple_of((u + 2) * PW, PW)
         weight_ref[pl.ds(at, PW), PW : 2 * PW] = both
-        return carry
-
-    lax.fori_loop(0, extent + 1, step, 0)
+
+    def step(index, before):
+        u = 2 * index
+        now = circulant(u)
+        after = circulant(u + 1)
+        place(u, now, before)
+        place(u + 1, after, now)
+        return after
+
+    lax.fori_loop(0, (extent + 1) // 2, step, jnp.zeros((PW, PW), F32))
 
 
 def build_windows(source_ref, window_ref, first, count):
@@ -108,20 +113,31 @@
 
 def step_kernel(
     n,
+    row_shift_hbm,
+    column_shift_hbm,
+    piece_width_hbm,
+    route_tile_hbm,
+    route_cell_hbm,
+    exposure_hbm,
+    row_fraction_hbm,
+    column_fraction_hbm,
+    template_hbm,
+    match_kernel_hbm,
+    detection_kernel_hbm,
+    difference,
+    significance,
+    noise_out,
     row_shift,
     column_shift,
     piece_width,
     route_tile,
     route_cell,
-    exposure,
     row_fraction,
     column_fraction,
     template,
     match_kernel,
     detection_kernel,
-    difference,
-    significance,
-    noise_out,
+    chosen,
     extended,
     warped,
     outgoing,
@@ -132,11 +148,11 @@
     match_weight,
     detect_weight,
     taps,
-    taps64,
     total,
     rounded,
     window2,
     partials,
+    load_sem,
     halo_send,
     halo_recv,
     piece_send,
@@ -144,10 +160,30 @@
     noise_send,
     noise_recv,
 ):
+    height, columns = exposure_hbm.shape
+    loads = [
+        pltpu.make_async_copy(a, b, load_sem.at[k])
+        for k, (a, b) in enumerate(
+            [
+                (exposure_hbm, extended.at[0:height]),
+                (route_tile_hbm, route_tile),
+                (route_cell_hbm, route_cell),
+                (piece_width_hbm, piece_width),
+                (row_shift_hbm, row_shift),
+                (column_shift_hbm, column_shift),
+                (row_fraction_hbm, row_fraction),
+                (column_fraction_hbm, column_fraction),
+                (template_hbm, template),
+                (match_kernel_hbm, match_kernel),
+                (detection_kernel_hbm, detection_kernel),
+            ]
+        )
+    ]
+    for load in loads:
+        load.start()
     me = lax.axis_index("ccd")
     band = lax.axis_index("row")
     partner = 1 - band
-    height, columns = exposure.shape
     pieces = columns // PW
     cells = template.shape[0] // height
     margin = match_kernel.shape[0] // 2
@@ -177,23 +213,15 @@
 
     lax.fori_loop(1, everyone, greet, 0)
 
-    extended[0:height, :] = exposure[...]
     outer = jnp.zeros((margin, cells, PW), BF16)
     source[pl.ds(band * (height + margin), margin)] = outer
-    for r in range(height):
-        tiles[r] = template[pl.ds(r // 8 * cells * 8 + r % 8, cells, stride=8), :].astype(BF16)
-    source[margin : margin + height] = tiles[...]
     for q in (0, 1, rows2 // QUAD - 2, rows2 // QUAD - 1):
         rounded[q * QUAD : (q + 1) * QUAD] = jnp.zeros((QUAD, cells, PW), BF16)
-    build_weights(detection_kernel, taps, taps64, detect_weight)
-    build_weights(match_kernel, taps, taps64, match_weight)
-    build_windows(source, window, margin // QUAD, quads)
-    build_windows(source, window, band * ((height + margin) // QUAD), margin // QUAD)
-
+    loads[0].wait()
     pl.semaphore_wait(barrier, everyone - 1)
 
     exposure_copy = pltpu.make_async_remote_copy(
-        src_ref=exposure.at[0:HALO],
+        src_ref=extended.at[0:HALO],
         dst_ref=extended.at[height : height + HALO],
         send_sem=halo_send.at[0],
         recv_sem=halo_recv.at[0],
@@ -201,15 +229,22 @@
         device_id_type=MESH,
     )
     exposure_copy.start()
-    template_copy = pltpu.make_async_remote_copy(
-        src_ref=tiles.at[pl.ds(partner * (height - margin), margin)],
-        dst_ref=source.at[pl.ds(band * (height + margin), margin)],
-        send_sem=halo_send.at[1],
-        recv_sem=halo_recv.at[1],
-        device_id={"row": partner},
-        device_id_type=MESH,
-    )
-    template_copy.start()
+    for load in loads[1:8]:
+        load.wait()
+
+    def choose(index, carry):
+        tile = along(index)
+        first = pieces
+        second = pieces
+        for p in reversed(range(pieces)):
+            here = route_tile[0, p] == tile
+            second = jnp.where(here, first, second)
+            first = jnp.where(here, p, first)
+        chosen[index, 0] = first
+        chosen[index, 1] = second
+        return carry
+
+    lax.fori_loop(0, n, choose, 0)
 
     exposure_copy.wait()
     below = extended[height : height + HALO, :]
@@ -262,15 +297,8 @@
         ).astype(BF16)
 
     def pack(index, carry):
-        tile = along(index)
-        first = pieces
-        second = pieces
-        for p in reversed(range(pieces)):
-            here = route_tile[0, p] == tile
-            second = jnp.where(here, first, second)
-            first = jnp.where(here, p, first)
-        outgoing[index, 0] = warped[first]
-        outgoing[index, 1] = warped[second]
+        for k in range(PAIR):
+            outgoing[index, k] = warped[chosen[index, k]]
         return carry
 
     lax.fori_loop(0, n, pack, 0)
@@ -292,9 +320,27 @@
     lax.fori_loop(1, n, send_piece, 0)
     incoming[0] = outgoing[0]
 
+    for load in loads[8:]:
+        load.wait()
+    for r in range(height):
+        tiles[r] = template[pl.ds(r // 8 * cells * 8 + r % 8, cells, stride=8), :].astype(BF16)
+    template_copy = pltpu.make_async_remote_copy(
+        src_ref=tiles.at[pl.ds(partner * (height - margin), margin)],
+        dst_ref=source.at[pl.ds(band * (height + margin), margin)],
+        send_sem=halo_send.at[1],
+        recv_sem=halo_recv.at[1],
+        device_id={"row": partner},
+        device_id_type=MESH,
+    )
+    template_copy.start()
+    source[margin : margin + height] = tiles[...]
+    build_weights(match_kernel, taps, match_weight)
+    build_windows(source, window, margin // QUAD, quads)
+    build_windows(source, window, band * ((height + margin) // QUAD), margin // QUAD)
     template_copy.wait()
     build_windows(source, window, partner * ((height + margin) // QUAD), margin // QUAD)
     run_filter(window, match_weight, total, match_kernel.shape[0], quads, 0)
+    build_weights(detection_kernel, taps, detect_weight)
 
     def take_piece(index, carry):
         piece_copy(index).wait_recv()
@@ -344,16 +390,6 @@
         rounded[lead + r] = d.astype(BF16)
     partials[0] = jnp.sum(squares.reshape(cells // 8, 8, PW), axis=0)
 
-    difference_copy = pltpu.make_async_remote_copy(
-        src_ref=rounded.at[pl.ds(lead + partner * (height - margin2), margin2)],
-        dst_ref=rounded.at[pl.ds(lead - margin2 + band * (height + margin2), margin2)],
-        send_sem=halo_send.at[2],
-        recv_sem=halo_recv.at[2],
-        device_id={"row": partner},
-        device_id_type=MESH,
-    )
-    difference_copy.start()
-
     def noise_copy(index):
         return pltpu.make_async_remote_copy(
             src_ref=partials.at[0],
@@ -369,6 +405,16 @@
         return carry
 
     lax.fori_loop(1, everyone, send_noise, 0)
+
+    difference_copy = pltpu.make_async_remote_copy(
+        src_ref=rounded.at[pl.ds(lead + partner * (height - margin2), margin2)],
+        dst_ref=rounded.at[pl.ds(lead - margin2 + band * (height + margin2), margin2)],
+        send_sem=halo_send.at[2],
+        recv_sem=halo_recv.at[2],
+        device_id={"row": partner},
+        device_id_type=MESH,
+    )
+    difference_copy.start()
 
     build_windows(rounded, window2, lead // QUAD, quads)
     build_windows(rounded, window2, band * ((height + lead) // QUAD), lead // QUAD)
@@ -424,7 +470,7 @@
     extent2 = detection_kernel.shape[1]
     rows = height + 2 * (extent // 2)
     rows2 = height + 2 * QUAD * -(-(extent2 // 2) // QUAD)
-    smem = pl.BlockSpec(memory_space=pltpu.SMEM)
+    anywhere = pl.BlockSpec(memory_space=pl.ANY)
     vmem = pl.BlockSpec(memory_space=pltpu.VMEM)
     tiles = template.reshape(height // 8, 8, cells, PW).transpose(0, 2, 1, 3).reshape(height * cells, PW)
     difference, significance, noise = pl.pallas_call(
@@ -434,9 +480,20 @@
             jax.ShapeDtypeStruct((height * cells, PW), F32),
             jax.ShapeDtypeStruct((1, 1), F32),
         ),
-        in_specs=[smem] * 5 + [vmem] * 6,
+        in_specs=[anywhere] * 11,
         out_specs=(vmem, vmem, vmem),
         scratch_shapes=[
+            pltpu.SMEM(row_shift.shape, jnp.int32),
+            pltpu.SMEM(column_shift.shape, jnp.int32),
+            pltpu.SMEM(piece_width.shape, jnp.int32),
+            pltpu.SMEM(route_tile.shape, jnp.int32),
+            pltpu.SMEM(route_cell.shape, jnp.int32),
+            pltpu.VMEM(row_fraction.shape, BF16),
+            pltpu.VMEM(column_fraction.shape, BF16),
+            pltpu.VMEM((height * cells, PW), F32),
+            pltpu.VMEM((extent, extent), BF16),
+            pltpu.VMEM((extent2, extent2), BF16),
+            pltpu.SMEM((n, PAIR), jnp.int32),
             pltpu.VMEM((height + HALO, columns), F32),
             pltpu.VMEM((pieces + 1, SLOT, PW), BF16),
             pltpu.VMEM((n, PAIR, SLOT, PW), BF16),
@@ -447,11 +504,11 @@
             pltpu.VMEM(((extent + QUAD - 1) * PW, 2 * PW), BF16),
             pltpu.VMEM(((extent2 + QUAD - 1) * PW, 2 * PW), BF16),
             pltpu.VMEM((extent + 15, PW), F32),
-            pltpu.VMEM((extent + 15, PW), F32),
             pltpu.VMEM((height // QUAD * 2 * cells, 2 * PW), F32),
             pltpu.VMEM((rows2, cells, PW), BF16),
             pltpu.VMEM((rows2 // QUAD, QUAD, 2 * cells, PW), BF16),
             pltpu.VMEM((2 * n, 8, PW), F32),
+            pltpu.SemaphoreType.DMA((11,)),
             pltpu.SemaphoreType.DMA((3,)),
             pltpu.SemaphoreType.DMA((3,)),
             pltpu.SemaphoreType.DMA((n,)),
@@ -460,7 +517,7 @@
             pltpu.SemaphoreType.DMA((2 * n,)),
         ],
         compiler_params=pltpu.CompilerParams(
-            collective_id=0, has_side_effects=True, vmem_limit_bytes=40 * 2**20
+            collective_id=0, has_side_effects=True, vmem_limit_bytes=62 * 2**20
         ),
     )(
         row_shift,

time: 37.7 us -> 31.3 us (0.83)
  Pallas kernels: 28.1 us -> 24.8 us
  local copies, waits for them, and re-layouts: 5.47 us -> 2.57 us
    pallas_call x1, Pallas kernels: 28.1 us -> 24.8 us  [on_device(): pl.pallas_call(functools.partial(step_kernel, n), out_shape=(jax.ShapeDty...]
    unnamed x20 -> x4, local copies, waits for them, and re-layouts: 5.47 us -> 2.57 us
where the time goes in v3:
time: 31.3 us; the launch traced here: 31.1 us
  Pallas kernels  24.8 us (79%)
  between operations  3.71 us (12%)
  local copies, waits for them, and re-layouts  2.57 us (8%)
    pallas_call x1, Pallas kernels, on_device(): pl.pallas_call(functools.partial(step_kernel, n), out_shape=(jax.ShapeDty...  24.8 us
    unnamed x4, local copies, waits for them, and re-layouts  2.57 us

profile of v3, /device:TPU:0, one launch (start us, length us, event | category | flops | bytes accessed | tf_op | source)
XLA Modules:
  0.0 31.1 jit_solution(15921555448681696479)
XLA Ops:
  1.9 24.8 %shard_map.130 = (f32[768,128]{1,0:T(8,128)}, f32[768,128]{1,0:T(8,128)}, f32[1,1]{1,0:T(1,128)}) custom-call(s32[1]{0:T(128)S(6)} %copy.17.row_shift_hbm, s32[1]{0:T(128)S(6)} %copy.18.column_shift_hbm, s32[1,16]{1,0:T(1,128)} %piece_width_hbm.1, s32[1,16]{1,0:T(1,128)} %route_tile_hbm.1, s32[1,16]{1,0:T(1,128)} %route_cell_hbm.1, f32[24,2048]{1,0:T(8,128)} %bitcast.22, ...), custom_call_target="tpu_custom_call" | custom-call | tf_op jit(solution)/shard_map/pallas_call | solution.py:476
  26.8 0.0 copy-start
  26.8 1.8 %copy.19 = f32[1,24,4096]{2,1,0:T(8,128)} copy(f32[1,24,4096]{2,1,0:T(8,128)} %bitcast.21) | data formatting | bytes 786432
  28.6 0.0 copy-done
  28.6 0.7 %copy.20 = f32[1,24,4096]{2,1,0:T(8,128)} copy(f32[1,24,4096]{2,1,0:T(8,128)S(1)} %bitcast.20) | data formatting | bytes 786432
Async XLA Ops:
  26.8 1.8 %copy-start = (f32[768,128]{1,0:T(8,128)S(1)}, f32[768,128]{1,0:T(8,128)}, u32[]{:S(2)}) copy-start(f32[768,128]{1,0:T(8,128)} %get-tuple-element.7) | copy-start | bytes 1179652

commit v4 on v3

--- a/solution.py
+++ b/solution.py
@@ -388,12 +388,12 @@
         difference[pl.ds(r // 8 * cells * 8 + r % 8, cells, stride=8), :] = d
         squares = squares + d * d
         rounded[lead + r] = d.astype(BF16)
-    partials[0] = jnp.sum(squares.reshape(cells // 8, 8, PW), axis=0)
+    partials[0, 0:1] = jnp.sum(squares, axis=0, keepdims=True)
 
     def noise_copy(index):
         return pltpu.make_async_remote_copy(
-            src_ref=partials.at[0],
-            dst_ref=partials.at[index],
+            src_ref=partials.at[0, 0:1],
+            dst_ref=partials.at[index, 0:1],
             send_sem=noise_send.at[index],
             recv_sem=noise_recv.at[index],
             device_id=peer(index),
@@ -434,7 +434,7 @@
 
     lax.fori_loop(1, n, end_piece, 0)
 
-    squares = jnp.sum(partials[...], axis=0)
+    squares = jnp.sum(partials[:, 0:1, :], axis=0)
     square_sum = jnp.sum(jnp.sum(squares, axis=0, keepdims=True), axis=1, keepdims=True)
     live_count = live_total[:, 0:1] * float(2 * height)
     noise = square_sum / live_count

time: 31.3 us -> 31.3 us (level)
  no operation moved by 1% of the time
where the time goes in v4:
time: 31.3 us; the launch traced here: 31.1 us
  Pallas kernels  24.8 us (79%)
  between operations  3.71 us (12%)
  local copies, waits for them, and re-layouts  2.57 us (8%)
    pallas_call x1, Pallas kernels, on_device(): pl.pallas_call(functools.partial(step_kernel, n), out_shape=(jax.ShapeDty...  24.8 us
    unnamed x4, local copies, waits for them, and re-layouts  2.57 us

profile of v4, /device:TPU:0, one launch (start us, length us, event | category | flops | bytes accessed | tf_op | source)
XLA Modules:
  0.0 31.1 jit_solution(14020921816247384180)
XLA Ops:
  1.9 24.8 %shard_map.130 = (f32[768,128]{1,0:T(8,128)}, f32[768,128]{1,0:T(8,128)}, f32[1,1]{1,0:T(1,128)}) custom-call(s32[1]{0:T(128)S(6)} %copy.17.row_shift_hbm, s32[1]{0:T(128)S(6)} %copy.18.column_shift_hbm, s32[1,16]{1,0:T(1,128)} %piece_width_hbm.1, s32[1,16]{1,0:T(1,128)} %route_tile_hbm.1, s32[1,16]{1,0:T(1,128)} %route_cell_hbm.1, f32[24,2048]{1,0:T(8,128)} %bitcast.22, ...), custom_call_target="tpu_custom_call" | custom-call | tf_op jit(solution)/shard_map/pallas_call | solution.py:476
  26.8 0.0 copy-start
  26.8 1.8 %copy.19 = f32[1,24,4096]{2,1,0:T(8,128)} copy(f32[1,24,4096]{2,1,0:T(8,128)} %bitcast.21) | data formatting | bytes 786432
  28.6 0.0 copy-done
  28.6 0.7 %copy.20 = f32[1,24,4096]{2,1,0:T(8,128)} copy(f32[1,24,4096]{2,1,0:T(8,128)S(1)} %bitcast.20) | data formatting | bytes 786432
Async XLA Ops:
  26.8 1.8 %copy-start = (f32[768,128]{1,0:T(8,128)S(1)}, f32[768,128]{1,0:T(8,128)}, u32[]{:S(2)}) copy-start(f32[768,128]{1,0:T(8,128)} %get-tuple-element.7) | copy-start | bytes 1179652
